TPU v7x, 8 devices: a whole 2x2x1 slice. The times are simulated.
8 devices in a mesh: fsdp: 4 (over z, y, x), tp: 2 (over core).
Axes of the slice: x: 2, y: 2, z: 1, core: 2. Of those that a mesh axis runs over, the one named last changes fastest.
Arguments:
- x: bfloat16 [32768, 2560], P(('fsdp', 'tp'))
- gamma: float32 [2560], replicated
- w1: bfloat16 [2560, 10240], P('fsdp', 'tp')
- w2: bfloat16 [10240, 2560], P('tp', 'fsdp')
Outputs:
- output: bfloat16 [32768, 2560], P(('fsdp', 'tp'))
All inputs are finite; a program needn't handle non-finite values.
Results may differ from a plain program's by a relative error of at most 0.001.
Values are sent between devices in bfloat16 or wider.
A program may use at most 1 GiB of HBM per device.

v0:
```python
import jax
import jax.numpy as jnp
from jax import lax
from jax.sharding import PartitionSpec as P

EPS = 1e-6


def _norm(x, gamma):
    xf = x.astype(jnp.float32)
    mu = jnp.mean(xf, axis=-1, keepdims=True)
    var = jnp.mean(jnp.square(xf - mu), axis=-1, keepdims=True)
    return xf, ((xf - mu) * lax.rsqrt(var + EPS) * gamma).astype(jnp.bfloat16)


def solution(mesh):
    def body(x, gamma, w1, w2):
        w1f = lax.all_gather(w1, "fsdp", axis=0, tiled=True)
        w2f = lax.all_gather(w2, "fsdp", axis=1, tiled=True)
        xf, xn = _norm(x, gamma)
        xg = lax.all_gather(xn, "tp", axis=0, tiled=True)
        h = jax.nn.gelu(jnp.dot(xg, w1f, preferred_element_type=jnp.float32), approximate=True).astype(jnp.bfloat16)
        yp = jnp.dot(h, w2f, preferred_element_type=jnp.float32)
        y = lax.psum_scatter(yp, "tp", scatter_dimension=0, tiled=True)
        return (xf + y).astype(jnp.bfloat16)

    return jax.shard_map(
        body,
        mesh=mesh,
        in_specs=(P(("fsdp", "tp"), None), P(None), P("fsdp", "tp"), P("tp", "fsdp")),
        out_specs=P(("fsdp", "tp"), None),
        check_vma=False,
    )
```

profile of v0, /device:TPU:0, one launch (start us, length us, event | category | flops | bytes accessed | tf_op | source)
XLA Modules:
  0.0 899.5 jit_solution(5832201479384361381)
XLA Ops:
  6.5 0.0 copy-start
  6.5 0.0 all-gather.6.cloned.1.call-start
  6.5 0.7 all-gather.6.cloned.1.call-update
  7.3 0.0 all-gather.4.cloned.1.call-start
  7.3 0.0 slice-start
  7.3 0.0 slice-start.1
  7.3 0.0 slice-start.2
  7.3 11.0 %convert_reduce_fusion = f32[4096]{0:T(1024)S(1)} fusion(bf16[4096,2560]{1,0:T(8,128)(2,1)} %param.4), kind=kLoop, calls=%fused_computation.12 | loop fusion | flops 20967424 | bytes 20987904 | tf_op jit(solution)/shard_map/reduce_sum | solution.py:11
  18.4 0.0 slice-start.3
  18.4 0.0 slice-start.4
  18.4 12.2 %fusion.12 = f32[4096]{0:T(1024)S(1)} fusion(bf16[4096,2560]{1,0:T(8,128)(2,1)} %param.4, f32[4096]{0:T(1024)S(1)} %broadcast_multiply_fusion), kind=kLoop, calls=%fused_computation.15 | loop fusion | flops 41938944 | bytes 21004288 | tf_op jit(solution)/shard_map/reduce_sum | solution.py:12
  30.6 0.0 copy-done
  30.6 0.0 slice-done
  30.6 0.0 slice-done.1
  30.6 0.0 slice-done.2
  30.7 0.0 slice-done.3
  30.7 0.0 slice-done.4
  30.7 11.3 %fusion.14 = bf16[4096,2560]{1,0:T(8,128)(2,1)} fusion(bf16[4096,2560]{1,0:T(8,128)(2,1)S(1)} %bitcast.6, f32[2560]{0:T(1024)S(1)} %copy-done, f32[4096]{0:T(1024)S(1)} %add_rsqrt_fusion, f32[4096]{0:T(1024)S(1)} %broadcast_multiply_fusion), kind=kLoop, calls=%fused_computation.17 | loop fusion | flops 52428800 | bytes 41986048 | tf_op jit(solution)/shard_map/convert_element_type | solution.py:13
  42.0 0.0 all-gather.4.cloned.1.call-update
  42.0 0.0 all-gather.8.cloned.1.call-start
  42.0 0.7 all-gather.8.cloned.1.call-update
  42.7 0.0 reduce-scatter.5.cloned.1.call-start
  42.8 200.0 %all-gather.6.cloned.1.call-done = bf16[2560,5120]{1,0:T(8,128)(2,1)} async-done(((bf16[640,5120]{1,0:T(8,128)(2,1)}), bf16[2560,5120]{1,0:T(8,128)(2,1)}) %all-gather.6.cloned.1.call-update) | async-done | bytes 26214416 | tf_op jit(solution)/shard_map/all_gather | solution.py:18
  242.7 60.2 %all-gather.4.cloned.1.call-done = bf16[8192,2560]{1,0:T(8,128)(2,1)} async-done(((bf16[4096,2560]{1,0:T(8,128)(2,1)}), bf16[8192,2560]{1,0:T(8,128)(2,1)}) %all-gather.4.cloned.1.call-update) | async-done | bytes 41943056 | tf_op jit(solution)/shard_map/all_gather | solution.py:21
  302.9 230.9 %fusion.20 = f32[8192,5120]{1,0:T(8,128)} fusion(bf16[8192,2560]{1,0:T(8,128)(2,1)} %all-gather.4.cloned.1.call-done, bf16[2560,5120]{1,0:T(8,128)(2,1)} %all-gather.6.cloned.1.call-done), kind=kOutput, calls=%fused_computation.25 | convolution fusion | flops 214748364800 | bytes 235929600 | tf_op jit(solution)/shard_map/dot_general | solution.py:22
  533.8 2.8 all-gather.8.cloned.1.call-done
  536.7 244.5 %fusion.8 = f32[8192,2560]{1,0:T(8,128)} fusion(bf16[5120,2560]{1,0:T(8,128)(2,1)} %all-gather.8.cloned.1.call-done, f32[8192,5120]{1,0:T(8,128)} %fusion.20), kind=kOutput, calls=%fused_computation.9 | convolution fusion | flops 215125852160 | bytes 277872640 | tf_op jit(solution)/shard_map/dot_general | solution.py:23
  781.1 0.0 reduce-scatter.5.cloned.1.call-update
  781.2 84.2 %reduce-scatter.5.cloned.1.call-done = f32[4096,2560]{1,0:T(8,128)} async-done(((f32[8192,2560]{1,0:T(8,128)}), f32[4096,2560]{1,0:T(8,128)}) %reduce-scatter.5.cloned.1.call-update) | async-done | bytes 41943056
  865.3 27.6 %fusion.15 = bf16[4096,2560]{1,0:T(8,128)(2,1)} fusion(f32[4096,2560]{1,0:T(8,128)} %reduce-scatter.5.cloned.1.call-done, bf16[4096,2560]{1,0:T(8,128)(2,1)} %param.4), kind=kLoop, calls=%fused_computation.18 | loop fusion | flops 31457280 | bytes 83886080 | tf_op jit(solution)/shard_map/convert_element_type | solution.py:25
  (3 shorter events, 0.0 us)
Async XLA Ops:
  6.5 24.1 %copy-start = (f32[2560]{0:T(1024)S(1)}, f32[2560]{0:T(1024)}, u32[]{:S(2)}) copy-start(f32[2560]{0:T(1024)} %param.5) | copy-start | bytes 30724
  6.5 236.2 %all-gather.6.cloned.1.call-start = ((), (), s32[]{:S(2)}) async-start(), calls=%async_computation.2 | async-start | bytes 32768000 | tf_op jit(solution)/shard_map/all_gather | solution.py:18
  7.3 295.7 %all-gather.4.cloned.1.call-start = ((), (), s32[]{:S(2)}) async-start(), calls=%async_computation.1 | async-start | bytes 62914560 | tf_op jit(solution)/shard_map/all_gather | solution.py:21
  7.3 23.3 %slice-start = ((s8[20971520]{0:T(1024)(128)(4,1)}), s8[4194304]{0:T(1024)(128)(4,1)S(1)}, s32[]{:S(2)}) async-start(s8[20971520]{0:T(1024)(128)(4,1)} %bitcast.5), calls=%async_computation.5 | async-start | bytes 8388608
  7.3 23.3 %slice-start.1 = ((s8[20971520]{0:T(1024)(128)(4,1)}), s8[4194304]{0:T(1024)(128)(4,1)S(1)}, s32[]{:S(2)}) async-start(s8[20971520]{0:T(1024)(128)(4,1)} %bitcast.5), calls=%async_computation.6 | async-start | bytes 8388608
  7.3 23.3 %slice-start.2 = ((s8[20971520]{0:T(1024)(128)(4,1)}), s8[4194304]{0:T(1024)(128)(4,1)S(1)}, s32[]{:S(2)}) async-start(s8[20971520]{0:T(1024)(128)(4,1)} %bitcast.5), calls=%async_computation.7 | async-start | bytes 8388608
  18.4 12.3 %slice-start.3 = ((s8[20971520]{0:T(1024)(128)(4,1)}), s8[4194304]{0:T(1024)(128)(4,1)S(1)}, s32[]{:S(2)}) async-start(s8[20971520]{0:T(1024)(128)(4,1)} %bitcast.5), calls=%async_computation.8 | async-start | bytes 8388608
  18.4 12.3 %slice-start.4 = ((s8[20971520]{0:T(1024)(128)(4,1)}), s8[4194304]{0:T(1024)(128)(4,1)S(1)}, s32[]{:S(2)}) async-start(s8[20971520]{0:T(1024)(128)(4,1)} %bitcast.5), calls=%async_computation.9 | async-start | bytes 8388608
  42.0 494.7 %all-gather.8.cloned.1.call-start = ((), (), s32[]{:S(2)}) async-start(), calls=%async_computation.3 | async-start | bytes 32768000 | tf_op jit(solution)/shard_map/all_gather | solution.py:19
  42.7 822.6 %reduce-scatter.5.cloned.1.call-start = ((), (), s32[]{:S(2)}) async-start(), calls=%async_computation.4 | async-start | bytes 125829120
Sparse Core Ops, SparseCore 0:
  9.1 233.5 all-gather.5
  244.2 58.6 all-gather.3
  304.7 231.9 all-gather.7
  781.3 84.0 reduce-scatter.4
where the time goes:
time: 900 us
  matrix products  475 us (53%)
  waiting for transfers between devices  349 us (39%)
  other arithmetic  62.1 us (7%)
  between operations  13.3 us (1%)
    dot_general x1, matrix products, body(): yp = jnp.dot(h, w2f, preferred_element_type=jnp.float32)  244 us
    dot_general x1, matrix products, body(): jnp.dot(xg, w1f, preferred_element_type=jnp.float32)  231 us
    all_gather x1, waiting for transfers between devices, body(): w1f = lax.all_gather(w1, 'fsdp', axis=0, tiled=True)  200 us
    unnamed x5, waiting for transfers between devices  85.6 us
    all_gather x1, waiting for transfers between devices, body(): xg = lax.all_gather(xn, 'tp', axis=0, tiled=True)  60.2 us
    convert_element_type x1, other arithmetic, body(): return (xf + y).astype(jnp.bfloat16)  27.6 us
  transfers between devices with their start and end apart: 4, of which 4 were waited for; matrix products, arithmetic and copies ran while one was open for 30% of the time, Pallas kernels for 0%

commit v1 on v0

v1 whole, which is shorter than its diff:
```python
import functools

import jax
import jax.numpy as jnp
from jax import lax
from jax.experimental import pallas as pl
from jax.experimental.pallas import tpu as pltpu
from jax.sharding import PartitionSpec as P

EPS = 1e-6
MESH = pl.DeviceIdType.MESH
BF16 = jnp.bfloat16
F32 = jnp.float32

TOK = 4096
D = 2560
F = 10240
FH = F // 2
DS = D // 4
CH = 256
N1 = FH // CH
NK = 2 * N1
R1 = 1024
S1 = 256
R2 = 512
C2 = 512
K2 = 2 * CH
NS = FH // K2
EXTRA = 6

C0 = 0.7978845608028654
C1 = C0 * 0.044715


def _gelu(x):
    hx = 0.5 * x
    return hx + hx * jnp.tanh(x * (C0 + C1 * (x * x)))


def _kernel(x, gamma, w1, w2, y, h, g1, g2, xs, w2t, sems, wsem, bsem):
    a, b = lax.axis_index("fsdp"), lax.axis_index("tp")
    ax = a + 1 - 2 * lax.rem(a, 2)
    ay = a + 2 - 4 * lax.div(a, 2)
    ad = 3 - a
    chips = (a, ax, ay, ad)
    to_x, to_y, to_c = (ax, b), (ay, b), (a, 1 - b)

    def rows1(k, half):
        cols = pl.ds(pl.multiple_of(k * CH, CH), CH)
        if half is None:
            return (slice(None), cols)
        return (pl.ds(half * (DS // 2), DS // 2), cols)

    def rows2(k, half):
        if half is None:
            return (pl.ds(pl.multiple_of((k - N1) * CH, CH), CH), slice(None))
        hc = CH // 2
        return (pl.ds(pl.multiple_of((k - N1) * CH + half * hc, hc), hc), slice(None))

    class Links:
        def __init__(self, w, g, view):
            self.w, self.g, self.view = w, g, view

        def copy(self, kind, k, src, dst, half, dev):
            v = self.view(k, half)
            s = self.w.at[v] if src is None else self.g.at[(*src, *v)]
            return pltpu.make_async_remote_copy(
                src_ref=s,
                dst_ref=self.g.at[(*dst, *v)],
                send_sem=sems.at[0, kind, k],
                recv_sem=sems.at[1, kind, k],
                device_id=dev,
                device_id_type=MESH,
            )

        def direct(self, k):
            return [
                self.copy(0, k, None, (0, 1), None, to_x),
                self.copy(1, k, None, (0, 2), None, to_y),
            ]

        def forward(self, k):
            return [
                self.copy(2, k, (0, 2), (0, 3), 1, to_x),
                self.copy(3, k, (0, 1), (0, 3), 0, to_y),
            ]

        def core_own(self, k):
            return [self.copy(4, k, None, (1, 0), None, to_c)]

        def core_xy(self, k):
            return [
                self.copy(5, k, (0, 1), (1, 1), None, to_c),
                self.copy(6, k, (0, 2), (1, 2), None, to_c),
            ]

        def core_diag(self, k):
            return [self.copy(7, k, (0, 3), (1, 3), None, to_c)]

    L1, L2 = Links(w1, g1, rows1), Links(w2, g2, rows2)

    def start(copies):
        for c in copies:
            c.start()

    def arrived(copies):
        for c in copies:
            c.wait_recv()

    def ev_direct(ln, k):
        start(ln.direct(k))
        start(ln.core_own(k))

    def ev_forward(ln, k):
        arrived(ln.direct(k))
        start(ln.forward(k))
        start(ln.core_xy(k))

    def ev_diag(ln, k):
        arrived(ln.forward(k))
        start(ln.core_diag(k))

    def ev_here(ln, k):
        arrived(ln.core_own(k) + ln.core_xy(k) + ln.core_diag(k))

    def either(ev, k):
        @pl.when(k < N1)
        def _():
            ev(L1, k)

        @pl.when((k >= N1) & (k < NK))
        def _():
            ev(L2, k)

    def second(ev, k):
        @pl.when(k < NK)
        def _():
            ev(L2, k)

    def half_cols(half, start_col, n):
        off = (b if half == 0 else 1 - b) * FH + start_col
        return pl.ds(pl.multiple_of(off, n), n)

    def load_w2(s):
        slot = lax.rem(s, 2)
        v = (pl.ds(pl.multiple_of(s * K2, K2), K2), slice(None))
        for half in range(2):
            for r in range(4):
                src = w2.at[v] if half == 0 and r == 0 else g2.at[(half, r, *v)]
                cols = pl.ds(pl.multiple_of(chips[r] * DS, 128), DS)
                dst = w2t.at[slot, pl.ds(half * K2, K2), cols]
                pltpu.make_async_copy(src, dst, wsem.at[slot]).start()

    def wait_w2(s):
        slot = lax.rem(s, 2)
        whole = h.at[pl.ds(0, 2 * K2), pl.ds(0, D)]
        pltpu.make_async_copy(whole, w2t.at[slot], wsem.at[slot]).wait()

    def x_block(i):
        return x.at[pl.ds(pl.multiple_of(i * R2, R2), R2), :]

    def x_copy(i):
        slot = lax.rem(i, 2)
        return pltpu.make_async_copy(x_block(i), xs.at[slot], bsem.at[0, slot])

    barrier = pltpu.get_barrier_semaphore()
    for dev in (to_x, to_y, to_c):
        pl.semaphore_signal(barrier, inc=1, device_id=dev, device_id_type=MESH)
    x_copy(0).start()
    pl.semaphore_wait(barrier, 3)
    ev_direct(L1, 0)

    def first(xn, w1t, ht, lsem, osem):
        def load_w1(c):
            slot = lax.rem(c, 2)
            v = rows1(c, None)
            for half in range(2):
                for r in range(4):
                    src = w1.at[v] if half == 0 and r == 0 else g1.at[(half, r, *v)]
                    rows = pl.ds(pl.multiple_of(chips[r] * DS, 128), DS)
                    dst = w1t.at[slot, rows, pl.ds(half * CH, CH)]
                    pltpu.make_async_copy(src, dst, lsem.at[slot]).start()

        def wait_w1(c):
            slot = lax.rem(c, 2)
            whole = h.at[pl.ds(0, D), pl.ds(0, 2 * CH)]
            pltpu.make_async_copy(whole, w1t.at[slot], lsem.at[slot]).wait()

        def norm(i, _):
            slot = lax.rem(i, 2)

            @pl.when(i + 1 < TOK // R2)
            def _():
                x_copy(i + 1).start()

            x_copy(i).wait()

            def group(j, _):
                r = pl.ds(pl.multiple_of(j * 16, 16), 16)
                xf = xs[slot, r, :].astype(F32)
                mu = jnp.mean(xf, axis=-1, keepdims=True)
                d = xf - mu
                var = jnp.mean(d * d, axis=-1, keepdims=True)
                o = pl.ds(pl.multiple_of(i * R2 + j * 16, 16), 16)
                xn[o, :] = (d * lax.rsqrt(var + EPS) * gamma[...]).astype(BF16)
                return 0

            lax.fori_loop(0, R2 // 16, group, 0, unroll=4)

            @pl.when(i == 4)
            def _():
                ev_forward(L1, 0)
                ev_direct(L1, 1)
                ev_direct(L1, 2)

            return 0

        lax.fori_loop(0, TOK // R2, norm, 0)
        ev_diag(L1, 0)
        ev_here(L1, 0)
        load_w1(0)

        def out_copies(i):
            slot = lax.rem(i, 2)
            c, m = lax.div(i, 4), lax.rem(i, 4)
            r = pl.ds(pl.multiple_of(m * R1, R1), R1)
            return [
                pltpu.make_async_copy(
                    ht.at[slot, :, pl.ds(half * CH, CH)],
                    h.at[r, half_cols(half, c * CH, CH)],
                    osem.at[slot],
                )
                for half in range(2)
            ]

        def wait_out(i):
            slot = lax.rem(i, 2)
            whole = h.at[pl.ds(0, R1), pl.ds(0, 2 * CH)]
            pltpu.make_async_copy(ht.at[slot], whole, osem.at[slot]).wait()

        def step(i, _):
            c, m = lax.div(i, 4), lax.rem(i, 4)
            slot = lax.rem(i, 2)
            k = c + 1 + lax.div(c, EXTRA)
            more = lax.rem(c, EXTRA) == EXTRA - 1

            @pl.when(m == 0)
            def _():
                wait_w1(c)
                either(ev_forward, k)
                either(ev_direct, k + 2)

            @pl.when((m == 1) & more)
            def _():
                either(ev_forward, k + 1)
                either(ev_direct, k + 3)

            @pl.when(m == 2)
            def _():
                either(ev_diag, k)

            @pl.when(m == 3)
            def _():
                @pl.when(more)
                def _():
                    either(ev_diag, k + 1)

                @pl.when(c + 1 < N1)
                def _():
                    ev_here(L1, c + 1)
                    load_w1(c + 1)

                @pl.when(c + 1 == N1)
                def _():
                    ev_here(L2, N1)
                    ev_here(L2, N1 + 1)
                    load_w2(0)

            @pl.when(i >= 2)
            def _():
                wait_out(i)

            w = w1t.at[lax.rem(c, 2)]
            for j in range(R1 // S1):
                r = pl.ds(pl.multiple_of(m * R1 + j * S1, S1), S1)
                t = jnp.dot(xn[r, :], w[...], preferred_element_type=F32)
                ht[slot, j * S1 : (j + 1) * S1, :] = _gelu(t).astype(BF16)
            start(out_copies(i))
            return 0

        lax.fori_loop(0, 4 * N1, step, 0)
        wait_out(0)
        wait_out(1)

    pl.run_scoped(
        first,
        pltpu.VMEM((TOK, D), BF16),
        pltpu.VMEM((2, D, 2 * CH), BF16),
        pltpu.VMEM((2, R1, 2 * CH), BF16),
        pltpu.SemaphoreType.DMA((2,)),
        pltpu.SemaphoreType.DMA((2,)),
    )

    k_last = N1 + (N1 - 1) // EXTRA + (1 if N1 % EXTRA == 0 else 0)
    per = TOK // R2

    def rest(acc, ht, hsem):
        def load_h(i):
            slot = lax.rem(i, 2)
            s, m = lax.div(i, per), lax.rem(i, per)
            r = pl.ds(pl.multiple_of(m * R2, R2), R2)
            for half in range(2):
                pltpu.make_async_copy(
                    h.at[r, half_cols(half, s * K2, K2)],
                    ht.at[slot, :, pl.ds(half * K2, K2)],
                    hsem.at[slot],
                ).start()

        def wait_h(i):
            slot = lax.rem(i, 2)
            whole = h.at[pl.ds(0, R2), pl.ds(0, 2 * K2)]
            pltpu.make_async_copy(whole, ht.at[slot], hsem.at[slot]).wait()

        def y_copy(i):
            slot = lax.rem(i, 2)
            m = lax.rem(i, per)
            r = pl.ds(pl.multiple_of(m * R2, R2), R2)
            return pltpu.make_async_copy(xs.at[slot], y.at[r, :], bsem.at[1, slot])

        load_h(0)

        def step(mode, i, _):
            s, m = lax.div(i, per), lax.rem(i, per)
            slot = lax.rem(i, 2)
            k = k_last + 1 + 2 * s

            if mode != "last":
                for q, kk in ((0, k), (4, k + 1)):

                    @pl.when(m == q)
                    def _(kk=kk):
                        second(ev_forward, kk)
                        second(ev_direct, kk + 2)

                    @pl.when(m == q + 2)
                    def _(kk=kk):
                        second(ev_diag, kk)

            @pl.when(m == 0)
            def _():
                wait_w2(s)

            if mode != "last":

                @pl.when(m == per - 1)
                def _():
                    second(ev_here, N1 + 2 * s + 2)
                    second(ev_here, N1 + 2 * s + 3)
                    load_w2(s + 1)

            if mode == "last":

                @pl.when(m == 0)
                def _():
                    x_copy(0).start()

                @pl.when(m >= 1)
                def _():
                    y_copy(i - 1).wait()

                @pl.when(m + 1 < per)
                def _():
                    x_copy(m + 1).start()

            @pl.when(i + 1 < per * NS)
            def _():
                load_h(i + 1)

            wait_h(i)
            r = pl.ds(pl.multiple_of(m * R2, R2), R2)
            w = w2t.at[lax.rem(s, 2)]
            if mode == "last":
                x_copy(m).wait()
            for n in range(D // C2):
                cols = slice(n * C2, (n + 1) * C2)
                t = jnp.dot(ht[slot], w[:, cols], preferred_element_type=F32)
                if mode == "first":
                    acc[r, cols] = t
                elif mode == "mid":
                    acc[r, cols] += t
                else:
                    t = xs[slot, :, cols].astype(F32) + (acc[r, cols] + t)
                    xs[slot, :, cols] = t.astype(BF16)
            if mode == "last":
                y_copy(i).start()
            return 0

        lax.fori_loop(0, per, functools.partial(step, "first"), 0)
        lax.fori_loop(per, per * (NS - 1), functools.partial(step, "mid"), 0)
        lax.fori_loop(per * (NS - 1), per * NS, functools.partial(step, "last"), 0)
        y_copy(per * NS - 1).wait()

    pl.run_scoped(
        rest,
        pltpu.VMEM((TOK, D), F32),
        pltpu.VMEM((2, R2, 2 * K2), BF16),
        pltpu.SemaphoreType.DMA((2,)),
    )

    def drain(ln, k, _):
        for c in ln.direct(k) + ln.forward(k) + ln.core_own(k) + ln.core_xy(k) + ln.core_diag(k):
            c.wait_send()
        return 0

    lax.fori_loop(0, N1, functools.partial(drain, L1), 0)
    lax.fori_loop(N1, NK, functools.partial(drain, L2), 0)


def solution(mesh):
    any_ = pl.BlockSpec(memory_space=pl.ANY)

    def body(x, gamma, w1, w2):
        y, _, _, _ = pl.pallas_call(
            _kernel,
            out_shape=(
                jax.ShapeDtypeStruct((TOK, D), BF16),
                jax.ShapeDtypeStruct((TOK, F), BF16),
                jax.ShapeDtypeStruct((2, 4, DS, FH), BF16),
                jax.ShapeDtypeStruct((2, 4, FH, DS), BF16),
            ),
            in_specs=[any_, pl.BlockSpec(memory_space=pltpu.VMEM), any_, any_],
            out_specs=(any_,) * 4,
            scratch_shapes=[
                pltpu.VMEM((2, R2, D), BF16),
                pltpu.VMEM((2, 2 * K2, D), BF16),
                pltpu.SemaphoreType.DMA((2, 8, NK)),
                pltpu.SemaphoreType.DMA((2,)),
                pltpu.SemaphoreType.DMA((2, 2)),
            ],
            compiler_params=pltpu.CompilerParams(
                collective_id=0, has_side_effects=True, vmem_limit_bytes=67043328
            ),
            name="mlp",
        )(x, gamma.reshape(1, D), w1, w2)
        return y

    return jax.shard_map(
        body,
        mesh=mesh,
        in_specs=(P(("fsdp", "tp"), None), P(None), P("fsdp", "tp"), P("tp", "fsdp")),
        out_specs=P(("fsdp", "tp"), None),
        check_vma=False,
    )
```

time: 900 us -> 592 us (0.66)
  Pallas kernels: 0 us -> 573 us
  matrix products: 475 us -> 0 us
  waiting for transfers between devices: 349 us -> 0 us
  other arithmetic: 62.1 us -> 0 us
  local copies, waits for them, and re-layouts: 0.03 us -> 18.5 us
  between operations: 13.3 us -> 0.01 us
    pallas_call x0 -> x1, Pallas kernels: none -> 573 us  [body(): pl.pallas_call(_kernel, out_shape=(jax.ShapeDtypeStruct((TOK, D), BF16),...]
    dot_general x2 -> x0, matrix products: 475 us -> none  [the longest x1 244 us: body(): yp = jnp.dot(h, w2f, preferred_element_type=jnp.float32)]
    all_gather x3 -> x0, waiting for transfers between devices: 263 us -> none  [the longest x1 200 us: body(): w1f = lax.all_gather(w1, 'fsdp', axis=0, tiled=True)]
    unnamed x5 -> x0, waiting for transfers between devices: 85.6 us -> none
    convert_element_type x2 -> x0, other arithmetic: 38.9 us -> none  [the longest x1 27.6 us: body(): return (xf + y).astype(jnp.bfloat16)]
    reduce_sum x2 -> x0, other arithmetic: 23.2 us -> none  [the longest x1 12.2 us: _norm(): var = jnp.mean(jnp.square(xf - mu), axis=-1, keepdims=True)]
    unnamed x12 -> x1, local copies, waits for them, and re-layouts: 0.03 us -> 17.2 us
  transfers between devices with their start and end apart: 4 -> 0, of which waited for: 4 -> 0; matrix products, arithmetic and copies ran while one was open for 30% -> 0% of each run, Pallas kernels for 0% -> 0%
where the time goes in v1:
time: 592 us; the launch traced here: 591 us
  Pallas kernels  573 us (97%)
  local copies, waits for them, and re-layouts  18.5 us (3%)
    pallas_call x1, Pallas kernels, body(): pl.pallas_call(_kernel, out_shape=(jax.ShapeDtypeStruct((TOK, D), BF16),...  573 us
    unnamed x1, local copies, waits for them, and re-layouts  17.2 us

profile of v1, /device:TPU:0, one launch (start us, length us, event | category | flops | bytes accessed | tf_op | source)
XLA Modules:
  0.0 591.2 jit_solution(11694783193380333802)
XLA Ops:
  0.0 1.3 reshape.3.gamma
  1.3 572.7 %mlp.1 = (bf16[4096,2560]{1,0:T(8,128)(2,1)}, bf16[4096,10240]{1,0:T(8,128)(2,1)}, bf16[2,4,640,5120]{3,2,1,0:T(8,128)(2,1)}, bf16[2,4,5120,640]{3,2,1,0:T(8,128)(2,1)}) custom-call(bf16[4096,2560]{1,0:T(8,128)(2,1)} %x.1, f32[1,2560]{1,0:T(1,128)} %reshape.3.gamma, bf16[640,5120]{1,0:T(8,128)(2,1)} %w1.1, bf16[5120,640]{1,0:T(8,128)(2,1)} %w2.1), custom_call_target="tpu_custom_call" | custom-call | tf_op jit(solution)/shard_map/mlp/pallas_call | solution.py:423
  574.0 17.2 %copy.6 = bf16[4096,2560]{1,0:T(8,128)(2,1)} copy(bf16[4096,2560]{1,0:T(8,128)(2,1)} %get-tuple-element.6) | data formatting | bytes 41943040

commit v2 on v1

--- a/solution.py
+++ b/solution.py
@@ -22,10 +22,15 @@
 NK = 2 * N1
 R1 = 1024
 S1 = 256
-R2 = 512
+R2 = 1024
+S2 = 512
+RX = 512
+RG = 128
 C2 = 512
 K2 = 2 * CH
-NS = FH // K2
+NS = FH // K2 - 2
+RT = 512
+KT = FH - NS * K2
 EXTRA = 6
 
 C0 = 0.7978845608028654
@@ -37,7 +42,7 @@
     return hx + hx * jnp.tanh(x * (C0 + C1 * (x * x)))
 
 
-def _kernel(x, gamma, w1, w2, y, h, g1, g2, xs, w2t, sems, wsem, bsem):
+def _kernel(x, gamma, w1, w2, acc_out, h, g1, g2, w2t, sems, wsem):
     a, b = lax.axis_index("fsdp"), lax.axis_index("tp")
     ax = a + 1 - 2 * lax.rem(a, 2)
     ay = a + 2 - 4 * lax.div(a, 2)
@@ -156,21 +161,20 @@
         whole = h.at[pl.ds(0, 2 * K2), pl.ds(0, D)]
         pltpu.make_async_copy(whole, w2t.at[slot], wsem.at[slot]).wait()
 
-    def x_block(i):
-        return x.at[pl.ds(pl.multiple_of(i * R2, R2), R2), :]
-
-    def x_copy(i):
-        slot = lax.rem(i, 2)
-        return pltpu.make_async_copy(x_block(i), xs.at[slot], bsem.at[0, slot])
-
     barrier = pltpu.get_barrier_semaphore()
     for dev in (to_x, to_y, to_c):
         pl.semaphore_signal(barrier, inc=1, device_id=dev, device_id_type=MESH)
-    x_copy(0).start()
     pl.semaphore_wait(barrier, 3)
     ev_direct(L1, 0)
 
-    def first(xn, w1t, ht, lsem, osem):
+    def first(xn, xs, w1t, ht, late, xsem, lsem, osem):
+        def x_copy(i):
+            slot = lax.rem(i, 2)
+            r = pl.ds(pl.multiple_of(i * RX, RX), RX)
+            return pltpu.make_async_copy(x.at[r, :], xs.at[slot], xsem.at[slot])
+
+        x_copy(0).start()
+
         def load_w1(c):
             slot = lax.rem(c, 2)
             v = rows1(c, None)
@@ -189,25 +193,34 @@
         def norm(i, _):
             slot = lax.rem(i, 2)
 
-            @pl.when(i + 1 < TOK // R2)
+            @pl.when(i + 1 < TOK // RX)
             def _():
                 x_copy(i + 1).start()
 
             x_copy(i).wait()
 
             def group(j, _):
-                r = pl.ds(pl.multiple_of(j * 16, 16), 16)
-                xf = xs[slot, r, :].astype(F32)
-                mu = jnp.mean(xf, axis=-1, keepdims=True)
-                d = xf - mu
-                var = jnp.mean(d * d, axis=-1, keepdims=True)
-                o = pl.ds(pl.multiple_of(i * R2 + j * 16, 16), 16)
-                xn[o, :] = (d * lax.rsqrt(var + EPS) * gamma[...]).astype(BF16)
+                r = pl.ds(pl.multiple_of(j * RG, RG), RG)
+                o = pl.ds(pl.multiple_of(i * RX + j * RG, RG), RG)
+                tiles = [slice(n * 128, (n + 1) * 128) for n in range(D // 128)]
+                t = jnp.zeros((RG, 128), F32)
+                for n in tiles:
+                    t += xs[slot, r, n].astype(F32)
+                mu = jnp.sum(t, axis=-1, keepdims=True) * (1.0 / D)
+                t = jnp.zeros((RG, 128), F32)
+                for n in tiles:
+                    d = xs[slot, r, n].astype(F32) - mu
+                    t += d * d
+                var = jnp.sum(t, axis=-1, keepdims=True) * (1.0 / D)
+                rs = lax.rsqrt(var + EPS)
+                for n in tiles:
+                    d = xs[slot, r, n].astype(F32) - mu
+                    xn[o, n] = (d * rs * gamma[:, n]).astype(BF16)
                 return 0
 
-            lax.fori_loop(0, R2 // 16, group, 0, unroll=4)
-
-            @pl.when(i == 4)
+            lax.fori_loop(0, RX // RG, group, 0)
+
+            @pl.when(i == 3)
             def _():
                 ev_forward(L1, 0)
                 ev_direct(L1, 1)
@@ -215,7 +228,7 @@
 
             return 0
 
-        lax.fori_loop(0, TOK // R2, norm, 0)
+        lax.fori_loop(0, TOK // RX, norm, 0)
         ev_diag(L1, 0)
         ev_here(L1, 0)
         load_w1(0)
@@ -238,32 +251,51 @@
             whole = h.at[pl.ds(0, R1), pl.ds(0, 2 * CH)]
             pltpu.make_async_copy(ht.at[slot], whole, osem.at[slot]).wait()
 
+        late[...] = jnp.zeros_like(late)
+        top = R1 - S1
+
         def step(i, _):
             c, m = lax.div(i, 4), lax.rem(i, 4)
             slot = lax.rem(i, 2)
-            k = c + 1 + lax.div(c, EXTRA)
+            lead = lax.div(c, EXTRA)
             more = lax.rem(c, EXTRA) == EXTRA - 1
+            k = c + 1 + lead
+            g = c + 1 + jnp.maximum(lead - 1, 0)
 
             @pl.when(m == 0)
             def _():
                 wait_w1(c)
                 either(ev_forward, k)
-                either(ev_direct, k + 2)
+
+                @pl.when(c <= EXTRA)
+                def _():
+                    either(ev_direct, k + 2)
+
+                @pl.when(c >= EXTRA)
+                def _():
+                    either(ev_direct, k + 3)
 
             @pl.when((m == 1) & more)
             def _():
                 either(ev_forward, k + 1)
-                either(ev_direct, k + 3)
+
+                @pl.when(c < EXTRA)
+                def _():
+                    either(ev_direct, k + 3)
+
+                @pl.when(c > EXTRA)
+                def _():
+                    either(ev_direct, k + 4)
 
             @pl.when(m == 2)
             def _():
-                either(ev_diag, k)
+                either(ev_diag, g)
 
             @pl.when(m == 3)
             def _():
-                @pl.when(more)
-                def _():
-                    either(ev_diag, k + 1)
+                @pl.when(more & (c > EXTRA))
+                def _():
+                    either(ev_diag, g + 1)
 
                 @pl.when(c + 1 < N1)
                 def _():
@@ -281,22 +313,38 @@
                 wait_out(i)
 
             w = w1t.at[lax.rem(c, 2)]
+            before = late[...]
             for j in range(R1 // S1):
                 r = pl.ds(pl.multiple_of(m * R1 + j * S1, S1), S1)
                 t = jnp.dot(xn[r, :], w[...], preferred_element_type=F32)
-                ht[slot, j * S1 : (j + 1) * S1, :] = _gelu(t).astype(BF16)
-            start(out_copies(i))
+                if j == 0:
+                    ht[1 - slot, top:, :] = _gelu(before).astype(BF16)
+                if j < R1 // S1 - 1:
+                    ht[slot, j * S1 : (j + 1) * S1, :] = _gelu(t).astype(BF16)
+                else:
+                    late[...] = t
+
+            @pl.when(i >= 1)
+            def _():
+                start(out_copies(i - 1))
+
             return 0
 
-        lax.fori_loop(0, 4 * N1, step, 0)
+        n = 4 * N1
+        lax.fori_loop(0, n, step, 0)
         wait_out(0)
+        ht[(n - 1) % 2, top:, :] = _gelu(late[...]).astype(BF16)
+        start(out_copies(n - 1))
         wait_out(1)
 
     pl.run_scoped(
         first,
         pltpu.VMEM((TOK, D), BF16),
+        pltpu.VMEM((2, RX, D), BF16),
         pltpu.VMEM((2, D, 2 * CH), BF16),
         pltpu.VMEM((2, R1, 2 * CH), BF16),
+        pltpu.VMEM((S1, 2 * CH), F32),
+        pltpu.SemaphoreType.DMA((2,)),
         pltpu.SemaphoreType.DMA((2,)),
         pltpu.SemaphoreType.DMA((2,)),
     )
@@ -304,7 +352,7 @@
     k_last = N1 + (N1 - 1) // EXTRA + (1 if N1 % EXTRA == 0 else 0)
     per = TOK // R2
 
-    def rest(acc, ht, hsem):
+    def rest(acc, ht, hsem, asem):
         def load_h(i):
             slot = lax.rem(i, 2)
             s, m = lax.div(i, per), lax.rem(i, per)
@@ -321,91 +369,81 @@
             whole = h.at[pl.ds(0, R2), pl.ds(0, 2 * K2)]
             pltpu.make_async_copy(whole, ht.at[slot], hsem.at[slot]).wait()
 
-        def y_copy(i):
-            slot = lax.rem(i, 2)
-            m = lax.rem(i, per)
+        def acc_copy(m):
             r = pl.ds(pl.multiple_of(m * R2, R2), R2)
-            return pltpu.make_async_copy(xs.at[slot], y.at[r, :], bsem.at[1, slot])
+            return pltpu.make_async_copy(acc.at[r, :], acc_out.at[r, :], asem.at[m])
 
         load_h(0)
 
-        def step(mode, i, _):
+        def step(first_slot, i, _):
             s, m = lax.div(i, per), lax.rem(i, per)
             slot = lax.rem(i, 2)
             k = k_last + 1 + 2 * s
 
-            if mode != "last":
-                for q, kk in ((0, k), (4, k + 1)):
-
-                    @pl.when(m == q)
-                    def _(kk=kk):
-                        second(ev_forward, kk)
-                        second(ev_direct, kk + 2)
-
-                    @pl.when(m == q + 2)
-                    def _(kk=kk):
-                        second(ev_diag, kk)
+            for q in range(2):
+
+                @pl.when(m == 2 * q)
+                def _(q=q):
+                    second(ev_forward, k + q)
+                    second(ev_direct, k + q + 3)
+
+                @pl.when(m == 2 * q + 1)
+                def _(q=q):
+                    second(ev_diag, k - 1 + q)
 
             @pl.when(m == 0)
             def _():
                 wait_w2(s)
 
-            if mode != "last":
-
-                @pl.when(m == per - 1)
-                def _():
-                    second(ev_here, N1 + 2 * s + 2)
-                    second(ev_here, N1 + 2 * s + 3)
-                    load_w2(s + 1)
-
-            if mode == "last":
-
-                @pl.when(m == 0)
-                def _():
-                    x_copy(0).start()
-
-                @pl.when(m >= 1)
-                def _():
-                    y_copy(i - 1).wait()
-
-                @pl.when(m + 1 < per)
-                def _():
-                    x_copy(m + 1).start()
+            @pl.when((m == per - 1) & (s + 1 < NS))
+            def _():
+                ev_here(L2, N1 + 2 * s + 2)
+                ev_here(L2, N1 + 2 * s + 3)
+                load_w2(s + 1)
 
             @pl.when(i + 1 < per * NS)
             def _():
                 load_h(i + 1)
 
             wait_h(i)
-            r = pl.ds(pl.multiple_of(m * R2, R2), R2)
             w = w2t.at[lax.rem(s, 2)]
-            if mode == "last":
-                x_copy(m).wait()
-            for n in range(D // C2):
-                cols = slice(n * C2, (n + 1) * C2)
-                t = jnp.dot(ht[slot], w[:, cols], preferred_element_type=F32)
-                if mode == "first":
-                    acc[r, cols] = t
-                elif mode == "mid":
-                    acc[r, cols] += t
-                else:
-                    t = xs[slot, :, cols].astype(F32) + (acc[r, cols] + t)
-                    xs[slot, :, cols] = t.astype(BF16)
-            if mode == "last":
-                y_copy(i).start()
+            for j in range(R2 // S2):
+                r = pl.ds(pl.multiple_of(m * R2 + j * S2, S2), S2)
+                for n in range(D // C2):
+                    cols = slice(n * C2, (n + 1) * C2)
+                    hj = ht[slot, j * S2 : (j + 1) * S2, :]
+                    t = jnp.dot(hj, w[:, cols], preferred_element_type=F32)
+                    if first_slot:
+                        acc[r, cols] = t
+                    else:
+                        acc[r, cols] += t
+
+            @pl.when(s == NS - 1)
+            def _():
+                acc_copy(m).start()
+
             return 0
 
-        lax.fori_loop(0, per, functools.partial(step, "first"), 0)
-        lax.fori_loop(per, per * (NS - 1), functools.partial(step, "mid"), 0)
-        lax.fori_loop(per * (NS - 1), per * NS, functools.partial(step, "last"), 0)
-        y_copy(per * NS - 1).wait()
+        lax.fori_loop(0, per, functools.partial(step, True), 0)
+        lax.fori_loop(per, per * NS, functools.partial(step, False), 0)
+        for m in range(per):
+            acc_copy(m).wait()
 
     pl.run_scoped(
         rest,
         pltpu.VMEM((TOK, D), F32),
         pltpu.VMEM((2, R2, 2 * K2), BF16),
         pltpu.SemaphoreType.DMA((2,)),
+        pltpu.SemaphoreType.DMA((per,)),
     )
+
+    ev_diag(L2, NK - 1)
+
+    def last(k, _):
+        ev_here(L2, k)
+        return 0
+
+    lax.fori_loop(N1 + 2 * NS, NK, last, 0)
 
     def drain(ln, k, _):
         for c in ln.direct(k) + ln.forward(k) + ln.core_own(k) + ln.core_xy(k) + ln.core_diag(k):
@@ -416,14 +454,37 @@
     lax.fori_loop(N1, NK, functools.partial(drain, L2), 0)
 
 
+def _tail(x, acc, h0, h1, w2, g2, y, wt, sem):
+    @pl.when(pl.program_id(0) == 0)
+    def _():
+        a, b = lax.axis_index("fsdp"), lax.axis_index("tp")
+        ax = a + 1 - 2 * lax.rem(a, 2)
+        ay = a + 2 - 4 * lax.div(a, 2)
+        chips = (a, ax, ay, 3 - a)
+        for half in range(2):
+            for r in range(4):
+                v = (pl.ds(FH - KT, KT), slice(None))
+                src = w2.at[v] if half == 0 and r == 0 else g2.at[(half, r, *v)]
+                rows = pl.ds(pl.multiple_of((b if half == 0 else 1 - b) * KT, KT), KT)
+                cols = pl.ds(pl.multiple_of(chips[r] * DS, 128), DS)
+                pltpu.make_async_copy(src, wt.at[rows, cols], sem).start()
+        pltpu.make_async_copy(wt, wt, sem).wait()
+
+    for n in range(D // C2):
+        cols = slice(n * C2, (n + 1) * C2)
+        t = jnp.dot(h0[...], wt[:KT, cols], preferred_element_type=F32)
+        t += jnp.dot(h1[...], wt[KT:, cols], preferred_element_type=F32)
+        y[:, cols] = (x[:, cols].astype(F32) + (acc[:, cols] + t)).astype(BF16)
+
+
 def solution(mesh):
     any_ = pl.BlockSpec(memory_space=pl.ANY)
 
     def body(x, gamma, w1, w2):
-        y, _, _, _ = pl.pallas_call(
+        acc, h, _, g2 = pl.pallas_call(
             _kernel,
             out_shape=(
-                jax.ShapeDtypeStruct((TOK, D), BF16),
+                jax.ShapeDtypeStruct((TOK, D), F32),
                 jax.ShapeDtypeStruct((TOK, F), BF16),
                 jax.ShapeDtypeStruct((2, 4, DS, FH), BF16),
                 jax.ShapeDtypeStruct((2, 4, FH, DS), BF16),
@@ -431,18 +492,32 @@
             in_specs=[any_, pl.BlockSpec(memory_space=pltpu.VMEM), any_, any_],
             out_specs=(any_,) * 4,
             scratch_shapes=[
-                pltpu.VMEM((2, R2, D), BF16),
                 pltpu.VMEM((2, 2 * K2, D), BF16),
                 pltpu.SemaphoreType.DMA((2, 8, NK)),
                 pltpu.SemaphoreType.DMA((2,)),
-                pltpu.SemaphoreType.DMA((2, 2)),
             ],
             compiler_params=pltpu.CompilerParams(
                 collective_id=0, has_side_effects=True, vmem_limit_bytes=67043328
             ),
             name="mlp",
         )(x, gamma.reshape(1, D), w1, w2)
-        return y
+        return pl.pallas_call(
+            _tail,
+            grid=(TOK // RT,),
+            out_shape=jax.ShapeDtypeStruct((TOK, D), BF16),
+            in_specs=[
+                pl.BlockSpec((RT, D), lambda m: (m, 0)),
+                pl.BlockSpec((RT, D), lambda m: (m, 0)),
+                pl.BlockSpec((RT, KT), lambda m: (m, FH // KT - 1)),
+                pl.BlockSpec((RT, KT), lambda m: (m, F // KT - 1)),
+                any_,
+                any_,
+            ],
+            out_specs=pl.BlockSpec((RT, D), lambda m: (m, 0)),
+            scratch_shapes=[pltpu.VMEM((2 * KT, D), BF16), pltpu.SemaphoreType.DMA],
+            compiler_params=pltpu.CompilerParams(vmem_limit_bytes=60 * 2**20),
+            name="tail",
+        )(x, acc, h, h, w2, g2)
 
     return jax.shard_map(
         body,

time: 592 us -> 609 us (1.029)
  Pallas kernels: 573 us -> 608 us
  local copies, waits for them, and re-layouts: 18.5 us -> 1.31 us
    pallas_call x1 -> x2, Pallas kernels: 573 us -> 608 us  [the longest x1 551 us: body(): pl.pallas_call(_kernel, out_shape=(jax.ShapeDtypeStruct((TOK, D), F32), j...]
    unnamed x1 -> x0, local copies, waits for them, and re-layouts: 17.2 us -> none
where the time goes in v2:
time: 609 us
  Pallas kernels  608 us (100%)
    pallas_call x1, Pallas kernels, body(): pl.pallas_call(_kernel, out_shape=(jax.ShapeDtypeStruct((TOK, D), F32), j...  551 us
    pallas_call x1, Pallas kernels, body(): pl.pallas_call(_tail, grid=(TOK // RT,), out_shape=jax.ShapeDtypeStruct((...  56.7 us

profile of v2, /device:TPU:0, one launch (start us, length us, event | category | flops | bytes accessed | tf_op | source)
XLA Modules:
  0.0 609.2 jit_solution(13922218122293044407)
XLA Ops:
  0.0 1.3 reshape.3.gamma
  1.3 551.0 %mlp.1 = (f32[4096,2560]{1,0:T(8,128)}, bf16[4096,10240]{1,0:T(8,128)(2,1)}, bf16[2,4,640,5120]{3,2,1,0:T(8,128)(2,1)}, bf16[2,4,5120,640]{3,2,1,0:T(8,128)(2,1)}) custom-call(bf16[4096,2560]{1,0:T(8,128)(2,1)} %x.3, f32[1,2560]{1,0:T(1,128)} %reshape.3.gamma, bf16[640,5120]{1,0:T(8,128)(2,1)} %w1.1, bf16[5120,640]{1,0:T(8,128)(2,1)} %w2.3), custom_call_target="tpu_custom_call" | custom-call | tf_op jit(solution)/shard_map/mlp/pallas_call | solution.py:484
  552.4 56.7 %tail.1 = bf16[4096,2560]{1,0:T(8,128)(2,1)} custom-call(bf16[4096,2560]{1,0:T(8,128)(2,1)} %x.3, f32[4096,2560]{1,0:T(8,128)} %get-tuple-element.8.acc, bf16[4096,10240]{1,0:T(8,128)(2,1)} %get-tuple-element.9.h0.h1, bf16[4096,10240]{1,0:T(8,128)(2,1)} %get-tuple-element.9.h0.h1, bf16[5120,640]{1,0:T(8,128)(2,1)} %w2.3, ...), custom_call_target="tpu_custom_call" | custom-call | tf_op jit(solution)/shard_map/tail/pallas_call | solution.py:504

commit v3 on v2

--- a/solution.py
+++ b/solution.py
@@ -20,7 +20,7 @@
 CH = 256
 N1 = FH // CH
 NK = 2 * N1
-R1 = 1024
+R1 = 2048
 S1 = 256
 R2 = 1024
 S2 = 512
@@ -167,7 +167,7 @@
     pl.semaphore_wait(barrier, 3)
     ev_direct(L1, 0)
 
-    def first(xn, xs, w1t, ht, late, xsem, lsem, osem):
+    def first(xn, xs, w1t, ht, xsem, lsem, osem):
         def x_copy(i):
             slot = lax.rem(i, 2)
             r = pl.ds(pl.multiple_of(i * RX, RX), RX)
@@ -233,109 +233,94 @@
         ev_here(L1, 0)
         load_w1(0)
 
-        def out_copies(i):
-            slot = lax.rem(i, 2)
-            c, m = lax.div(i, 4), lax.rem(i, 4)
-            r = pl.ds(pl.multiple_of(m * R1, R1), R1)
-            return [
-                pltpu.make_async_copy(
-                    ht.at[slot, :, pl.ds(half * CH, CH)],
-                    h.at[r, half_cols(half, c * CH, CH)],
-                    osem.at[slot],
-                )
-                for half in range(2)
-            ]
-
-        def wait_out(i):
-            slot = lax.rem(i, 2)
-            whole = h.at[pl.ds(0, R1), pl.ds(0, 2 * CH)]
-            pltpu.make_async_copy(ht.at[slot], whole, osem.at[slot]).wait()
-
-        late[...] = jnp.zeros_like(late)
-        top = R1 - S1
-
-        def step(i, _):
-            c, m = lax.div(i, 4), lax.rem(i, 4)
-            slot = lax.rem(i, 2)
-            lead = lax.div(c, EXTRA)
-            more = lax.rem(c, EXTRA) == EXTRA - 1
-            k = c + 1 + lead
-            g = c + 1 + jnp.maximum(lead - 1, 0)
-
-            @pl.when(m == 0)
-            def _():
-                wait_w1(c)
-                either(ev_forward, k)
-
-                @pl.when(c <= EXTRA)
+        def run(rows, c0, c1):
+            per = TOK // rows
+
+            def out_copies(i):
+                slot = lax.rem(i, 2)
+                c, m = c0 + lax.div(i, per), lax.rem(i, per)
+                r = pl.ds(pl.multiple_of(m * rows, rows), rows)
+                return [
+                    pltpu.make_async_copy(
+                        ht.at[slot, pl.ds(0, rows), pl.ds(half * CH, CH)],
+                        h.at[r, half_cols(half, c * CH, CH)],
+                        osem.at[slot],
+                    )
+                    for half in range(2)
+                ]
+
+            def wait_out(i):
+                slot = lax.rem(i, 2)
+                whole = h.at[pl.ds(0, rows), pl.ds(0, 2 * CH)]
+                done = ht.at[slot, pl.ds(0, rows)]
+                pltpu.make_async_copy(done, whole, osem.at[slot]).wait()
+
+            def step(i, _):
+                c, m = c0 + lax.div(i, per), lax.rem(i, per)
+                slot = lax.rem(i, 2)
+                lead = lax.div(c, EXTRA)
+                more = lax.rem(c, EXTRA) == EXTRA - 1
+                k = c + 1 + lead
+                g = c + 1 + jnp.maximum(lead - 1, 0)
+
+                @pl.when(m == 0)
                 def _():
-                    either(ev_direct, k + 2)
-
-                @pl.when(c >= EXTRA)
+                    wait_w1(c)
+                    if c0 > 0:
+                        either(ev_diag, g)
+                    either(ev_forward, k)
+                    if c0 == 0:
+                        either(ev_direct, k + 2)
+                    else:
+
+                        @pl.when(c == c0)
+                        def _():
+                            either(ev_direct, k + 2)
+
+                        either(ev_direct, k + 3)
+
+                @pl.when((m == 1) & more)
                 def _():
-                    either(ev_direct, k + 3)
-
-            @pl.when((m == 1) & more)
-            def _():
-                either(ev_forward, k + 1)
-
-                @pl.when(c < EXTRA)
-                def _():
-                    either(ev_direct, k + 3)
-
-                @pl.when(c > EXTRA)
-                def _():
-                    either(ev_direct, k + 4)
-
-            @pl.when(m == 2)
-            def _():
-                either(ev_diag, g)
-
-            @pl.when(m == 3)
-            def _():
-                @pl.when(more & (c > EXTRA))
-                def _():
-                    either(ev_diag, g + 1)
-
-                @pl.when(c + 1 < N1)
+                    either(ev_forward, k + 1)
+                    either(ev_direct, k + (3 if c0 == 0 else 4))
+                    if c0 > 0:
+                        either(ev_diag, g + 1)
+
+                if c0 == 0:
+
+                    @pl.when(m == 2)
+                    def _():
+                        either(ev_diag, g)
+
+                @pl.when((m == per - 1) & (c + 1 < N1))
                 def _():
                     ev_here(L1, c + 1)
                     load_w1(c + 1)
 
-                @pl.when(c + 1 == N1)
+                @pl.when((m == per - 1) & (c + 1 == N1))
                 def _():
                     ev_here(L2, N1)
                     ev_here(L2, N1 + 1)
                     load_w2(0)
 
-            @pl.when(i >= 2)
-            def _():
-                wait_out(i)
-
-            w = w1t.at[lax.rem(c, 2)]
-            before = late[...]
-            for j in range(R1 // S1):
-                r = pl.ds(pl.multiple_of(m * R1 + j * S1, S1), S1)
-                t = jnp.dot(xn[r, :], w[...], preferred_element_type=F32)
-                if j == 0:
-                    ht[1 - slot, top:, :] = _gelu(before).astype(BF16)
-                if j < R1 // S1 - 1:
+                @pl.when(i >= 2)
+                def _():
+                    wait_out(i)
+
+                w = w1t.at[lax.rem(c, 2)]
+                for j in range(rows // S1):
+                    r = pl.ds(pl.multiple_of(m * rows + j * S1, S1), S1)
+                    t = jnp.dot(xn[r, :], w[...], preferred_element_type=F32)
                     ht[slot, j * S1 : (j + 1) * S1, :] = _gelu(t).astype(BF16)
-                else:
-                    late[...] = t
-
-            @pl.when(i >= 1)
-            def _():
-                start(out_copies(i - 1))
-
-            return 0
-
-        n = 4 * N1
-        lax.fori_loop(0, n, step, 0)
-        wait_out(0)
-        ht[(n - 1) % 2, top:, :] = _gelu(late[...]).astype(BF16)
-        start(out_copies(n - 1))
-        wait_out(1)
+                start(out_copies(i))
+                return 0
+
+            lax.fori_loop(0, per * (c1 - c0), step, 0)
+            wait_out(0)
+            wait_out(1)
+
+        run(R1 // 2, 0, EXTRA)
+        run(R1, EXTRA, N1)
 
     pl.run_scoped(
         first,
@@ -343,7 +328,6 @@
         pltpu.VMEM((2, RX, D), BF16),
         pltpu.VMEM((2, D, 2 * CH), BF16),
         pltpu.VMEM((2, R1, 2 * CH), BF16),
-        pltpu.VMEM((S1, 2 * CH), F32),
         pltpu.SemaphoreType.DMA((2,)),
         pltpu.SemaphoreType.DMA((2,)),
         pltpu.SemaphoreType.DMA((2,)),

time: 609 us -> 549 us (0.901)
  Pallas kernels: 608 us -> 547 us
    pallas_call x1, Pallas kernels: 551 us -> 491 us  [body(): pl.pallas_call(_kernel, out_shape=(jax.ShapeDtypeStruct((TOK, D), F32), j...]
where the time goes in v3:
time: 549 us
  Pallas kernels  547 us (100%)
    pallas_call x1, Pallas kernels, body(): pl.pallas_call(_kernel, out_shape=(jax.ShapeDtypeStruct((TOK, D), F32), j...  491 us
    pallas_call x1, Pallas kernels, body(): pl.pallas_call(_tail, grid=(TOK // RT,), out_shape=jax.ShapeDtypeStruct((...  56.5 us

profile of v3, /device:TPU:0, one launch (start us, length us, event | category | flops | bytes accessed | tf_op | source)
XLA Modules:
  0.0 548.9 jit_solution(4288511527880839626)
XLA Ops:
  0.0 1.3 reshape.3.gamma
  1.3 490.9 %mlp.1 = (f32[4096,2560]{1,0:T(8,128)}, bf16[4096,10240]{1,0:T(8,128)(2,1)}, bf16[2,4,640,5120]{3,2,1,0:T(8,128)(2,1)}, bf16[2,4,5120,640]{3,2,1,0:T(8,128)(2,1)}) custom-call(bf16[4096,2560]{1,0:T(8,128)(2,1)} %x.3, f32[1,2560]{1,0:T(1,128)} %reshape.3.gamma, bf16[640,5120]{1,0:T(8,128)(2,1)} %w1.1, bf16[5120,640]{1,0:T(8,128)(2,1)} %w2.3), custom_call_target="tpu_custom_call" | custom-call | tf_op jit(solution)/shard_map/mlp/pallas_call | solution.py:468
  492.2 56.5 %tail.1 = bf16[4096,2560]{1,0:T(8,128)(2,1)} custom-call(bf16[4096,2560]{1,0:T(8,128)(2,1)} %x.3, f32[4096,2560]{1,0:T(8,128)} %get-tuple-element.8.acc, bf16[4096,10240]{1,0:T(8,128)(2,1)} %get-tuple-element.9.h0.h1, bf16[4096,10240]{1,0:T(8,128)(2,1)} %get-tuple-element.9.h0.h1, bf16[5120,640]{1,0:T(8,128)(2,1)} %w2.3, ...), custom_call_target="tpu_custom_call" | custom-call | tf_op jit(solution)/shard_map/tail/pallas_call | solution.py:488

commit v4 on v3

--- a/solution.py
+++ b/solution.py
@@ -42,7 +42,7 @@
     return hx + hx * jnp.tanh(x * (C0 + C1 * (x * x)))
 
 
-def _kernel(x, gamma, w1, w2, acc_out, h, g1, g2, w2t, sems, wsem):
+def _kernel(x, gamma, w1, w2, acc_out, h, g1, g2, w1t, w2t, ht, sems, wsem):
     a, b = lax.axis_index("fsdp"), lax.axis_index("tp")
     ax = a + 1 - 2 * lax.rem(a, 2)
     ay = a + 2 - 4 * lax.div(a, 2)
@@ -167,7 +167,7 @@
     pl.semaphore_wait(barrier, 3)
     ev_direct(L1, 0)
 
-    def first(xn, xs, w1t, ht, xsem, lsem, osem):
+    def first(xn, xs, xsem, lsem, osem):
         def x_copy(i):
             slot = lax.rem(i, 2)
             r = pl.ds(pl.multiple_of(i * RX, RX), RX)
@@ -239,21 +239,24 @@
             def out_copies(i):
                 slot = lax.rem(i, 2)
                 c, m = c0 + lax.div(i, per), lax.rem(i, per)
-                r = pl.ds(pl.multiple_of(m * rows, rows), rows)
                 return [
                     pltpu.make_async_copy(
-                        ht.at[slot, pl.ds(0, rows), pl.ds(half * CH, CH)],
-                        h.at[r, half_cols(half, c * CH, CH)],
+                        ht.at[slot, :, pl.ds(p * 2 * CH + half * CH, CH)],
+                        h.at[
+                            pl.ds(pl.multiple_of(m * rows + p * R2, R2), R2),
+                            half_cols(half, c * CH, CH),
+                        ],
                         osem.at[slot],
                     )
+                    for p in range(rows // R2)
                     for half in range(2)
                 ]
 
             def wait_out(i):
                 slot = lax.rem(i, 2)
-                whole = h.at[pl.ds(0, rows), pl.ds(0, 2 * CH)]
-                done = ht.at[slot, pl.ds(0, rows)]
-                pltpu.make_async_copy(done, whole, osem.at[slot]).wait()
+                cols = pl.ds(0, (rows // R2) * 2 * CH)
+                done = ht.at[slot, :, cols]
+                pltpu.make_async_copy(done, h.at[pl.ds(0, R2), cols], osem.at[slot]).wait()
 
             def step(i, _):
                 c, m = c0 + lax.div(i, per), lax.rem(i, per)
@@ -311,7 +314,9 @@
                 for j in range(rows // S1):
                     r = pl.ds(pl.multiple_of(m * rows + j * S1, S1), S1)
                     t = jnp.dot(xn[r, :], w[...], preferred_element_type=F32)
-                    ht[slot, j * S1 : (j + 1) * S1, :] = _gelu(t).astype(BF16)
+                    p, q = divmod(j * S1, R2)
+                    cols = slice(p * 2 * CH, (p + 1) * 2 * CH)
+                    ht[slot, q : q + S1, cols] = _gelu(t).astype(BF16)
                 start(out_copies(i))
                 return 0
 
@@ -326,8 +331,6 @@
         first,
         pltpu.VMEM((TOK, D), BF16),
         pltpu.VMEM((2, RX, D), BF16),
-        pltpu.VMEM((2, D, 2 * CH), BF16),
-        pltpu.VMEM((2, R1, 2 * CH), BF16),
         pltpu.SemaphoreType.DMA((2,)),
         pltpu.SemaphoreType.DMA((2,)),
         pltpu.SemaphoreType.DMA((2,)),
@@ -336,7 +339,7 @@
     k_last = N1 + (N1 - 1) // EXTRA + (1 if N1 % EXTRA == 0 else 0)
     per = TOK // R2
 
-    def rest(acc, ht, hsem, asem):
+    def rest(acc, hsem, asem):
         def load_h(i):
             slot = lax.rem(i, 2)
             s, m = lax.div(i, per), lax.rem(i, per)
@@ -416,7 +419,6 @@
     pl.run_scoped(
         rest,
         pltpu.VMEM((TOK, D), F32),
-        pltpu.VMEM((2, R2, 2 * K2), BF16),
         pltpu.SemaphoreType.DMA((2,)),
         pltpu.SemaphoreType.DMA((per,)),
     )
@@ -476,7 +478,9 @@
             in_specs=[any_, pl.BlockSpec(memory_space=pltpu.VMEM), any_, any_],
             out_specs=(any_,) * 4,
             scratch_shapes=[
+                pltpu.VMEM((2, D, 2 * CH), BF16),
                 pltpu.VMEM((2, 2 * K2, D), BF16),
+                pltpu.VMEM((2, R2, 2 * K2), BF16),
                 pltpu.SemaphoreType.DMA((2, 8, NK)),
                 pltpu.SemaphoreType.DMA((2,)),
             ],

time: 549 us -> 550 us (level)
  no operation moved by 1% of the time
where the time goes in v4:
time: 550 us; the launch traced here: 549 us
  Pallas kernels  548 us (100%)
    pallas_call x1, Pallas kernels, body(): pl.pallas_call(_kernel, out_shape=(jax.ShapeDtypeStruct((TOK, D), F32), j...  491 us
    pallas_call x1, Pallas kernels, body(): pl.pallas_call(_tail, grid=(TOK // RT,), out_shape=jax.ShapeDtypeStruct((...  56.5 us

profile of v4, /device:TPU:0, one launch (start us, length us, event | category | flops | bytes accessed | tf_op | source)
XLA Modules:
  0.0 549.4 jit_solution(16232335916672552745)
XLA Ops:
  0.0 1.3 reshape.3.gamma
  1.3 491.4 %mlp.1 = (f32[4096,2560]{1,0:T(8,128)}, bf16[4096,10240]{1,0:T(8,128)(2,1)}, bf16[2,4,640,5120]{3,2,1,0:T(8,128)(2,1)}, bf16[2,4,5120,640]{3,2,1,0:T(8,128)(2,1)}) custom-call(bf16[4096,2560]{1,0:T(8,128)(2,1)} %x.3, f32[1,2560]{1,0:T(1,128)} %reshape.3.gamma, bf16[640,5120]{1,0:T(8,128)(2,1)} %w1.1, bf16[5120,640]{1,0:T(8,128)(2,1)} %w2.3), custom_call_target="tpu_custom_call" | custom-call | tf_op jit(solution)/shard_map/mlp/pallas_call | solution.py:470
  492.7 56.5 %tail.1 = bf16[4096,2560]{1,0:T(8,128)(2,1)} custom-call(bf16[4096,2560]{1,0:T(8,128)(2,1)} %x.3, f32[4096,2560]{1,0:T(8,128)} %get-tuple-element.8.acc, bf16[4096,10240]{1,0:T(8,128)(2,1)} %get-tuple-element.9.h0.h1, bf16[4096,10240]{1,0:T(8,128)(2,1)} %get-tuple-element.9.h0.h1, bf16[5120,640]{1,0:T(8,128)(2,1)} %w2.3, ...), custom_call_target="tpu_custom_call" | custom-call | tf_op jit(solution)/shard_map/tail/pallas_call | solution.py:492

commit v5 on v4

--- a/solution.py
+++ b/solution.py
@@ -28,10 +28,10 @@
 RG = 128
 C2 = 512
 K2 = 2 * CH
-NS = FH // K2 - 2
+NS = FH // K2 - 1
 RT = 512
 KT = FH - NS * K2
-EXTRA = 6
+EXTRA = 7
 
 C0 = 0.7978845608028654
 C1 = C0 * 0.044715
@@ -367,16 +367,20 @@
             slot = lax.rem(i, 2)
             k = k_last + 1 + 2 * s
 
-            for q in range(2):
-
-                @pl.when(m == 2 * q)
-                def _(q=q):
-                    second(ev_forward, k + q)
-                    second(ev_direct, k + q + 3)
-
-                @pl.when(m == 2 * q + 1)
-                def _(q=q):
-                    second(ev_diag, k - 1 + q)
+            @pl.when(m == 0)
+            def _():
+                second(ev_diag, k - 1)
+                second(ev_forward, k)
+                second(ev_direct, k + 3)
+
+            @pl.when(m == 1)
+            def _():
+                second(ev_diag, k)
+
+            @pl.when(m == 2)
+            def _():
+                second(ev_forward, k + 1)
+                second(ev_direct, k + 4)
 
             @pl.when(m == 0)
             def _():
@@ -422,8 +426,6 @@
         pltpu.SemaphoreType.DMA((2,)),
         pltpu.SemaphoreType.DMA((per,)),
     )
-
-    ev_diag(L2, NK - 1)
 
     def last(k, _):
         ev_here(L2, k)

time: 550 us -> 552 us (level)
    pallas_call x1, Pallas kernels: 491 us -> 510 us  [body(): pl.pallas_call(_kernel, out_shape=(jax.ShapeDtypeStruct((TOK, D), F32), j...]
    pallas_call x1, Pallas kernels: 56.5 us -> 39.9 us  [body(): pl.pallas_call(_tail, grid=(TOK // RT,), out_shape=jax.ShapeDtypeStruct((...]
where the time goes in v5:
time: 552 us
  Pallas kernels  550 us (100%)
    pallas_call x1, Pallas kernels, body(): pl.pallas_call(_kernel, out_shape=(jax.ShapeDtypeStruct((TOK, D), F32), j...  510 us
    pallas_call x1, Pallas kernels, body(): pl.pallas_call(_tail, grid=(TOK // RT,), out_shape=jax.ShapeDtypeStruct((...  39.9 us

profile of v5, /device:TPU:0, one launch (start us, length us, event | category | flops | bytes accessed | tf_op | source)
XLA Modules:
  0.0 551.7 jit_solution(10108550627505675690)
XLA Ops:
  0.0 1.3 reshape.3.gamma
  1.3 510.3 %mlp.1 = (f32[4096,2560]{1,0:T(8,128)}, bf16[4096,10240]{1,0:T(8,128)(2,1)}, bf16[2,4,640,5120]{3,2,1,0:T(8,128)(2,1)}, bf16[2,4,5120,640]{3,2,1,0:T(8,128)(2,1)}) custom-call(bf16[4096,2560]{1,0:T(8,128)(2,1)} %x.3, f32[1,2560]{1,0:T(1,128)} %reshape.3.gamma, bf16[640,5120]{1,0:T(8,128)(2,1)} %w1.1, bf16[5120,640]{1,0:T(8,128)(2,1)} %w2.3), custom_call_target="tpu_custom_call" | custom-call | tf_op jit(solution)/shard_map/mlp/pallas_call | solution.py:472
  511.6 39.9 %tail.1 = bf16[4096,2560]{1,0:T(8,128)(2,1)} custom-call(bf16[4096,2560]{1,0:T(8,128)(2,1)} %x.3, f32[4096,2560]{1,0:T(8,128)} %get-tuple-element.8.acc, bf16[4096,10240]{1,0:T(8,128)(2,1)} %get-tuple-element.9.h0.h1, bf16[4096,10240]{1,0:T(8,128)(2,1)} %get-tuple-element.9.h0.h1, bf16[5120,640]{1,0:T(8,128)(2,1)} %w2.3, ...), custom_call_target="tpu_custom_call" | custom-call | tf_op jit(solution)/shard_map/tail/pallas_call | solution.py:494
